TPU v7x, 32 devices: a whole 2x2x4 slice. The times are simulated.
32 devices in a mesh: gx: 4 (over x, core), gy: 8 (over z, y).
Axes of the slice: x: 2, y: 2, z: 4, core: 2. Of those that a mesh axis runs over, the one named last changes fastest.
Arguments:
- fields: float32 [5, 32, 32, 1024], P(None, None, 'gx', 'gy'), may hold values from -20 to 20, as said below
- coriolis: float32 [32], P('gx'), may hold values from 0.5 to 1.5
- slope_east: float32 [32, 1024], P('gx', 'gy'), may hold values from -3 to 3
- slope_north: float32 [32, 1024], P('gx', 'gy'), may hold values from -3 to 3
Outputs:
- updated: float32 [4, 32, 32, 1024], P(None, None, 'gx', 'gy')
Inputs may be any that keep to these rules, and one draw needn't show every extreme that they name: `fields`: components in order: velocity along x, velocity along y, vertical velocity, potential temperature, pressure perturbation.
All inputs are finite; a program needn't handle non-finite values.
Results may differ from a plain program's by a relative error of at most 0.0003.
Values sent between devices are 32-bit elements; how exact they have to be, the bound alone decides.
A program may use at most 64 MiB of HBM per device.

v0:
```python
import jax
import jax.numpy as jnp
from jax import lax
from jax.sharding import PartitionSpec as P

WENO_EPS = 1e-06
SECTION_DT = 0.3
SMAG_COEF = 0.06
BACKGROUND = 0.05
BUOYANCY = 0.5


def padded(block, sides, width):
    for axis, dim in sides:
        count = lax.axis_size(axis)
        forward = [(i, i + 1) for i in range(count - 1)]
        backward = [(target, source) for source, target in forward]
        low = lax.ppermute(
            lax.slice_in_dim(block, block.shape[dim] - width, None, axis=dim), axis, forward
        )
        high = lax.ppermute(lax.slice_in_dim(block, 0, width, axis=dim), axis, backward)
        block = jnp.concatenate([low, block, high], axis=dim)
    return block


def window(array, start, length, axis):
    return lax.slice_in_dim(array, start, start + length, axis=axis)


def weno_face(outer_low, inner_low, middle, inner_high, outer_high):
    smooth_zero = (
        13.0 / 12.0 * (outer_low - 2.0 * inner_low + middle) ** 2
        + 0.25 * (outer_low - 4.0 * inner_low + 3.0 * middle) ** 2
    )
    smooth_one = (
        13.0 / 12.0 * (inner_low - 2.0 * middle + inner_high) ** 2
        + 0.25 * (inner_low - inner_high) ** 2
    )
    smooth_two = (
        13.0 / 12.0 * (middle - 2.0 * inner_high + outer_high) ** 2
        + 0.25 * (3.0 * middle - 4.0 * inner_high + outer_high) ** 2
    )
    guess_zero = (2.0 * outer_low - 7.0 * inner_low + 11.0 * middle) / 6.0
    guess_one = (-inner_low + 5.0 * middle + 2.0 * inner_high) / 6.0
    guess_two = (2.0 * middle + 5.0 * inner_high - outer_high) / 6.0
    weight_zero = 0.1 / (WENO_EPS + smooth_zero) ** 2
    weight_one = 0.6 / (WENO_EPS + smooth_one) ** 2
    weight_two = 0.3 / (WENO_EPS + smooth_two) ** 2
    total = weight_zero + weight_one + weight_two
    return (weight_zero * guess_zero + weight_one * guess_one + weight_two * guess_two) / total


def faces_along(values, speed, axis, count):
    parts = [window(values, offset, count + 1, axis) for offset in range(6)]
    low_side = weno_face(parts[0], parts[1], parts[2], parts[3], parts[4])
    high_side = weno_face(parts[5], parts[4], parts[3], parts[2], parts[1])
    face_speed = (window(speed, 2, count + 1, axis) + window(speed, 3, count + 1, axis)) * 0.5
    return jnp.maximum(face_speed, 0.0) * low_side + jnp.minimum(face_speed, 0.0) * high_side


def divergence(flux, axis, count):
    return window(flux, 1, count, axis) - window(flux, 0, count, axis)


def section_update(extended, pressure, coriolis, slope_east, slope_north, theta_mean):
    depth = extended.shape[1]
    rows = extended.shape[2] - 6
    cols = extended.shape[3] - 6
    centre = extended[:, :, 3:-3, 3:-3]
    along_x = extended[:, :, 3:-3, :]
    flux_x = faces_along(along_x, along_x[0:1], 3, cols)
    along_y = extended[:, :, :, 3:-3]
    flux_y = faces_along(along_y, along_y[1:2], 2, rows)
    padded_z = jnp.pad(centre, ((0, 0), (3, 3), (0, 0), (0, 0)), mode="edge")
    flux_z = faces_along(padded_z, padded_z[2:3], 1, depth)
    face_index = lax.broadcasted_iota(jnp.int32, (1, depth + 1, 1, 1), 1)
    inside = jnp.logical_and(face_index > 0, face_index < depth).astype(flux_z.dtype)
    flux_z = flux_z * inside
    advection = -(
        divergence(flux_x, 3, cols) + divergence(flux_y, 2, rows) + divergence(flux_z, 1, depth)
    )
    speed_x = extended[0]
    speed_y = extended[1]
    strain_xx = (speed_x[:, 2:-2, 3:-1] - speed_x[:, 2:-2, 1:-3]) * 0.5
    strain_yy = (speed_y[:, 3:-1, 2:-2] - speed_y[:, 1:-3, 2:-2]) * 0.5
    shear = (speed_x[:, 3:-1, 2:-2] - speed_x[:, 1:-3, 2:-2]) * 0.5 + (
        speed_y[:, 2:-2, 3:-1] - speed_y[:, 2:-2, 1:-3]
    ) * 0.5
    eddy = SMAG_COEF * jnp.sqrt(
        2.0 * (strain_xx * strain_xx + strain_yy * strain_yy) + shear * shear + BACKGROUND
    )
    border = extended[:, :, 2:-2, 2:-2]
    eddy_x = (eddy[:, 1:-1, 1:] + eddy[:, 1:-1, :-1]) * 0.5
    diffuse_x = eddy_x * (border[:, :, 1:-1, 1:] - border[:, :, 1:-1, :-1])
    eddy_y = (eddy[:, 1:, 1:-1] + eddy[:, :-1, 1:-1]) * 0.5
    diffuse_y = eddy_y * (border[:, :, 1:, 1:-1] - border[:, :, :-1, 1:-1])
    mixing = (
        diffuse_x[:, :, :, 1:]
        - diffuse_x[:, :, :, :-1]
        + diffuse_y[:, :, 1:, :]
        - diffuse_y[:, :, :-1, :]
    )
    press_x = (pressure[:, 1:-1, 2:] - pressure[:, 1:-1, :-2]) * 0.5
    press_y = (pressure[:, 2:, 1:-1] - pressure[:, :-2, 1:-1]) * 0.5
    column = jnp.pad(pressure[:, 1:-1, 1:-1], ((1, 1), (0, 0), (0, 0)), mode="edge")
    press_z = (column[2:] - column[:-2]) * 0.5
    level_index = lax.broadcasted_iota(jnp.int32, (depth, 1, 1), 0).astype(centre.dtype)
    level_factor = 1.0 - (level_index + 0.5) / depth
    turning = coriolis[None, :, None]
    force_u = -(press_x - slope_east[None] * level_factor * press_z) + turning * centre[1]
    force_v = -(press_y - slope_north[None] * level_factor * press_z) - turning * centre[0]
    force_w = -press_z + BUOYANCY * (centre[3] - theta_mean[:, None, None])
    forcing = jnp.stack([force_u, force_v, force_w, jnp.zeros_like(force_w)])
    return centre + SECTION_DT * (advection + mixing + forcing)


def body(fields, coriolis, slope_east, slope_north):
    level_total = lax.psum(jnp.sum(fields[3], axis=(1, 2)), ("gx", "gy"))
    cells = fields.shape[2] * fields.shape[3] * lax.axis_size("gx") * lax.axis_size("gy")
    theta_mean = level_total / cells
    widened = padded(fields, (("gy", 3),), 3)
    extended = padded(widened, (("gx", 2),), 3)
    pressure = extended[4, :, 2:-2, 2:-2]
    advected = extended[:4]
    return section_update(advected, pressure, coriolis, slope_east, slope_north, theta_mean)


def solution(mesh):
    return jax.shard_map(
        body,
        mesh=mesh,
        in_specs=(P(None, None, "gx", "gy"), P("gx"), P("gx", "gy"), P("gx", "gy")),
        out_specs=P(None, None, "gx", "gy"),
        check_vma=False,
    )
```

profile of v0, /device:TPU:1, one launch (start us, length us, event | category | flops | bytes accessed | tf_op | source)
XLA Modules:
  0.0 87.0 jit_solution(15989771767374200211)
XLA Ops:
  0.0 1.6 %fusion.140 = (f32[5,32,8,3]{3,2,1,0:T(8,128)S(1)}, f32[5,32,8,3]{3,2,1,0:T(8,128)S(1)}) fusion(f32[5,32,8,128]{3,2,1,0:T(8,128)} %param.4), kind=kLoop, calls=%fused_computation.217 | loop fusion | bytes 61440 | tf_op jit(solution)/shard_map/slice | solution.py:19
  1.6 0.3 copy.31
  1.9 4.0 %collective-permute-start = (f32[5,32,8,3]{1,2,3,0:T(8,128)S(1)}, f32[5,32,8,3]{1,2,3,0:T(8,128)S(1)}, u32[]{:S(2)}, u32[]{:S(2)}) collective-permute-start(f32[5,32,8,3]{1,2,3,0:T(8,128)S(1)} %copy.31), channel_id=1, source_target_pairs={{0,1},{1,2},{2,3},{3,4},{4,5},{5,6},{6,7},{8,9},{9,10},{10,11},{11... | collective-permute-start | bytes 46088 | tf_op jit(solution)/shard_map/ppermute | solution.py:18
  5.9 0.3 copy.32
  6.2 1.3 %collective-permute-start.1 = (f32[5,32,8,3]{1,2,3,0:T(8,128)S(1)}, f32[5,32,8,3]{1,2,3,0:T(8,128)S(1)}, u32[]{:S(2)}, u32[]{:S(2)}) collective-permute-start(f32[5,32,8,3]{1,2,3,0:T(8,128)S(1)} %copy.32), channel_id=1, source_target_pairs={{1,0},{2,1},{3,2},{4,3},{5,4},{6,5},{7,6},{9,8},{10,9},{11,10},{12... | collective-permute-start | bytes 46088 | tf_op jit(solution)/shard_map/ppermute | solution.py:21
  7.5 0.3 slice_reduce_fusion
  7.9 41.1 %psum.7 = f32[32]{0:T(128)S(1)} all-reduce(f32[32]{0:T(128)S(1)} %slice_reduce_fusion), channel_id=1, replica_groups=mesh['gx'=4,'gy'=8] {'gx','gy'}, use_global_device_ids=true, to_apply=%region_1.0 | all-reduce | flops 32 | bytes 256 | tf_op jit(solution)/shard_map/psum | solution.py:118
  49.1 2.8 %add_multiply_fusion = f32[4,33,8,128]{3,2,1,0:T(8,128)S(1)} fusion(f32[4,3,8,128]{3,2,1,0:T(8,128)S(1)} %reshape.41, f32[4,32,8,128]{3,2,1,0:T(8,128)S(1)} %slice.299, f32[4,3,8,128]{3,2,1,0:T(8,128)S(1)} %reshape.40, f32[33]{0:T(128)S(1)} %and_convert_fusion, f32[33,8,128]{2,1,0:T(8,128)S(1)} %minimum_bitcast_fusion.2, f32[33,8,128]{2,1,0:T(8,128)S(1)} %get-tuple-element.9), kind=kLoop, calls=%fused_computation.92 | loop fusion | flops 18112512 | bytes 1433732 | tf_op jit(solution)/shard_map/mul | solution.py:78
  52.0 0.3 copy.20
  52.3 0.3 copy.22
  52.7 0.6 pad_maximum_fusion.1
  53.5 5.3 %collective-permute-start.2 = (f32[5,32,3,134]{3,1,2,0:T(8,128)S(1)}, f32[5,32,3,134]{3,1,2,0:T(8,128)S(1)}, u32[]{:S(2)}, u32[]{:S(2)}) collective-permute-start(f32[5,32,3,134]{3,1,2,0:T(8,128)S(1)} %copy.25), channel_id=1, source_target_pairs={{0,8},{8,16},{16,24},{1,9},{9,17},{17,25},{2,10},{10,18},{18,26},{... | collective-permute-start | bytes 771848 | tf_op jit(solution)/shard_map/ppermute | solution.py:18
  58.9 2.1 %collective-permute-start.3 = (f32[5,32,3,134]{3,1,2,0:T(8,128)S(1)}, f32[5,32,3,134]{3,1,2,0:T(8,128)S(1)}, u32[]{:S(2)}, u32[]{:S(2)}) collective-permute-start(f32[5,32,3,134]{3,1,2,0:T(8,128)S(1)} %copy.27), channel_id=1, source_target_pairs={{8,0},{16,8},{24,16},{9,1},{17,9},{25,17},{10,2},{18,10},{26,18},{... | collective-permute-start | bytes 771848 | tf_op jit(solution)/shard_map/ppermute | solution.py:21
  61.2 3.3 %collective-permute-done.2 = f32[5,32,3,134]{3,1,2,0:T(8,128)S(1)} collective-permute-done((f32[5,32,3,134]{3,1,2,0:T(8,128)S(1)}, f32[5,32,3,134]{3,1,2,0:T(8,128)S(1)}, u32[]{:S(2)}, u32[]{:S(2)}) %collective-permute-start.2) | collective-permute-done | bytes 257312 | tf_op jit(solution)/shard_map/ppermute | solution.py:18
  64.6 0.3 copy.26
  64.9 4.2 %collective-permute-done.3 = f32[5,32,3,134]{3,1,2,0:T(8,128)S(1)} collective-permute-done((f32[5,32,3,134]{3,1,2,0:T(8,128)S(1)}, f32[5,32,3,134]{3,1,2,0:T(8,128)S(1)}, u32[]{:S(2)}, u32[]{:S(2)}) %collective-permute-start.3) | collective-permute-done | bytes 257312 | tf_op jit(solution)/shard_map/ppermute | solution.py:21
  69.1 0.3 copy.28
  69.4 0.5 fusion.95
  70.1 0.5 maximum_bitcast_fusion.1
  70.6 1.2 %fusion.106 = f32[32,10,130]{2,1,0:T(8,128)S(1)} fusion(f32[32,14,134]{2,1,0:T(8,128)S(1)} %get-tuple-element.14, f32[32,14,134]{2,1,0:T(8,128)S(1)} %get-tuple-element.13), kind=kLoop, calls=%fused_computation.154 | loop fusion | flops 665600 | bytes 1497600 | tf_op jit(solution)/shard_map/mul | solution.py:89
  72.4 1.8 %maximum_maximum_fusion = (f32[5,32,11,134]{3,2,1,0:T(8,128)S(1)}, f32[5,32,11,134]{3,2,1,0:T(8,128)S(1)}) fusion(f32[5,32,8,3]{3,2,1,0:T(8,128)S(1)} %copy.22, f32[5,32,8,128]{3,2,1,0:T(8,128)S(1)} %copy-done, f32[5,32,8,3]{3,2,1,0:T(8,128)S(1)} %copy.20, f32[5,32,3,134]{3,2,1,0:T(4,128)S(1)} %copy.26, f32[5,32,3,134]{3,2,1,0:T(4,128)S(1)} %copy.28), kind=kLoop, calls=%fused_computation | loop fusion | flops 1415040 | bytes 3087360 | tf_op jit(solution)/shard_map/concatenate | solution.py:22
  74.2 5.5 %multiply_add_fusion.3 = (f32[4,32,8,129]{3,2,1,0:T(8,128)S(1)}, f32[4,32,8,129]{3,2,1,0:T(8,128)S(1)}) fusion(f32[5,32,8,3]{3,2,1,0:T(8,128)S(1)} %copy.22, f32[5,32,8,128]{3,2,1,0:T(8,128)S(1)} %copy-done, f32[5,32,8,3]{3,2,1,0:T(8,128)S(1)} %copy.20, f32[32,8,129]{2,1,0:T(8,128)S(1)} %minimum_bitcast_fusion.1, f32[32,8,129]{2,1,0:T(8,128)S(1)} %get-tuple-element.5, ...), kind=kLoop, calls=%fused_computation.47 | loop fusion | flops 17965056 | bytes 2139136 | tf_op jit(solution)/shard_map/add | solution.py:58
  80.0 5.7 %multiply_add_fusion = (f32[4,32,9,128]{3,2,1,0:T(8,128)S(1)}, f32[4,32,9,128]{3,2,1,0:T(8,128)S(1)}) fusion(f32[5,32,11,134]{3,2,1,0:T(8,128)S(1)} %get-tuple-element.18, f32[5,32,11,134]{3,2,1,0:T(8,128)S(1)} %get-tuple-element.17, f32[32,9,128]{2,1,0:T(8,128)S(1)} %minimum_bitcast_fusion, f32[32,9,128]{2,1,0:T(8,128)S(1)} %get-tuple-element.7, ...), kind=kLoop, calls=%fused_computation.19 | loop fusion | flops 19021824 | bytes 5160960 | tf_op jit(solution)/shard_map/add | solution.py:58
  85.8 1.3 %fusion.99 = f32[4,32,8,128]{3,2,1,0:T(8,128)} fusion(f32[4,32,9,128]{3,2,1,0:T(8,128)S(1)} %get-tuple-element.12, f32[4,32,8,129]{3,2,1,0:T(8,128)S(1)} %get-tuple-element.16, f32[4,33,8,128]{3,2,1,0:T(8,128)S(1)} %add_multiply_fusion, f32[4,32,9,128]{3,2,1,0:T(8,128)S(1)} %get-tuple-element.11, f32[4,32,8,129]{3,2,1,0:T(8,128)S(1)} %get-tuple-element.15, ...), kind=kLoop, calls=%fused_computation.144 | loop fusion | flops 2097152 | bytes 6684688 | tf_op jit(solution)/shard_map/add | solution.py:114
  (33 shorter events, 1.9 us)
Async XLA Ops:
  0.0 7.5 %copy-start = (f32[5,32,8,128]{3,2,1,0:T(8,128)S(1)}, f32[5,32,8,128]{3,2,1,0:T(8,128)}, u32[]{:S(2)}) copy-start(f32[5,32,8,128]{3,2,1,0:T(8,128)} %param.4) | copy-start | bytes 1966084
  1.9 50.1 %collective-permute-start = (f32[5,32,8,3]{1,2,3,0:T(8,128)S(1)}, f32[5,32,8,3]{1,2,3,0:T(8,128)S(1)}, u32[]{:S(2)}, u32[]{:S(2)}) collective-permute-start(f32[5,32,8,3]{1,2,3,0:T(8,128)S(1)} %copy.31), channel_id=1, source_target_pairs={{0,1},{1,2},{2,3},{3,4},{4,5},{5,6},{6,7},{8,9},{9,10},{10,11},{11... | collective-permute-start | bytes 46088 | tf_op jit(solution)/shard_map/ppermute | solution.py:18
  6.2 46.1 %collective-permute-start.1 = (f32[5,32,8,3]{1,2,3,0:T(8,128)S(1)}, f32[5,32,8,3]{1,2,3,0:T(8,128)S(1)}, u32[]{:S(2)}, u32[]{:S(2)}) collective-permute-start(f32[5,32,8,3]{1,2,3,0:T(8,128)S(1)} %copy.32), channel_id=1, source_target_pairs={{1,0},{2,1},{3,2},{4,3},{5,4},{6,5},{7,6},{9,8},{10,9},{11,10},{12... | collective-permute-start | bytes 46088 | tf_op jit(solution)/shard_map/ppermute | solution.py:21
  53.5 11.0 %collective-permute-start.2 = (f32[5,32,3,134]{3,1,2,0:T(8,128)S(1)}, f32[5,32,3,134]{3,1,2,0:T(8,128)S(1)}, u32[]{:S(2)}, u32[]{:S(2)}) collective-permute-start(f32[5,32,3,134]{3,1,2,0:T(8,128)S(1)} %copy.25), channel_id=1, source_target_pairs={{0,8},{8,16},{16,24},{1,9},{9,17},{17,25},{2,10},{10,18},{18,26},{... | collective-permute-start | bytes 771848 | tf_op jit(solution)/shard_map/ppermute | solution.py:18
  58.9 10.1 %collective-permute-start.3 = (f32[5,32,3,134]{3,1,2,0:T(8,128)S(1)}, f32[5,32,3,134]{3,1,2,0:T(8,128)S(1)}, u32[]{:S(2)}, u32[]{:S(2)}) collective-permute-start(f32[5,32,3,134]{3,1,2,0:T(8,128)S(1)} %copy.27), channel_id=1, source_target_pairs={{8,0},{16,8},{24,16},{9,1},{17,9},{25,17},{10,2},{18,10},{26,18},{... | collective-permute-start | bytes 771848 | tf_op jit(solution)/shard_map/ppermute | solution.py:21
  74.2 5.6 %copy-start.1 = (f32[8,128]{1,0:T(8,128)S(1)}, f32[8,128]{1,0:T(8,128)}, u32[]{:S(2)}) copy-start(f32[8,128]{1,0:T(8,128)} %param.6) | copy-start | bytes 12292
  74.2 5.6 %copy-start.2 = (f32[8,128]{1,0:T(8,128)S(1)}, f32[8,128]{1,0:T(8,128)}, u32[]{:S(2)}) copy-start(f32[8,128]{1,0:T(8,128)} %param.7) | copy-start | bytes 12292
  74.2 5.6 %copy-start.3 = (f32[8]{0:T(128)S(1)}, f32[8]{0:T(128)}, u32[]{:S(2)}) copy-start(f32[8]{0:T(128)} %param.5) | copy-start | bytes 100
where the time goes:
time: 87.4 us; the launch traced here: 87 us
  blocking collectives  41.1 us (47%)
  other arithmetic  21.2 us (24%)
  starting transfers between devices  12.6 us (14%)
  waiting for transfers between devices  7.5 us (9%)
  local copies, waits for them, and re-layouts  4.28 us (5%)
    psum x1, blocking collectives, body(): level_total = lax.psum(jnp.sum(fields[3], axis=(1, 2)), ('gx', 'gy'))  41.1 us
    add x2, other arithmetic, faces_along(): jnp.maximum(face_speed, 0.0) * low_side  11.2 us
    ppermute x2, starting transfers between devices, padded(): lax.ppermute(lax.slice_in_dim(block, block.shape[dim] - width, None, axis...  9.24 us
    ppermute x2, waiting for transfers between devices, padded(): lax.ppermute(lax.slice_in_dim(block, 0, width, axis=dim), axis, backward)  4.15 us
    ppermute x2, starting transfers between devices, padded(): lax.ppermute(lax.slice_in_dim(block, 0, width, axis=dim), axis, backward)  3.39 us
    ppermute x2, waiting for transfers between devices, padded(): lax.ppermute(lax.slice_in_dim(block, block.shape[dim] - width, None, axis...  3.35 us
    mul x1, other arithmetic, section_update(): flux_z = flux_z * inside  2.81 us
    concatenate x2, other arithmetic, padded(): block = jnp.concatenate([low, block, high], axis=dim)  2.33 us
  transfers between devices with their start and end apart: 4, of which 2 were waited for; matrix products, arithmetic and copies ran while one was open for 5% of the time, Pallas kernels for 0%

commit v1 on v0

v1 whole, which is shorter than its diff:
```python
import functools

import jax
import jax.numpy as jnp
from jax import lax
from jax.experimental import pallas as pl
from jax.experimental.pallas import tpu as pltpu
from jax.sharding import PartitionSpec as P

WENO_EPS = 1e-06
SECTION_DT = 0.3
SMAG_COEF = 0.06
BACKGROUND = 0.05
BUOYANCY = 0.5
MESH = pl.DeviceIdType.MESH
HALF_DT = 0.5 * SECTION_DT
LANES = 128
ROWS = 8


def weno_flux(cells, positive, speed, weight):
    q0, q1, q2, q3, q4, q5 = cells
    d0, d1, d2, d3, d4 = q1 - q0, q2 - q1, q3 - q2, q4 - q3, q5 - q4
    e1 = jnp.where(positive, d0, d4)
    e2 = jnp.where(positive, d1, d3)
    e3 = d2
    e4 = jnp.where(positive, d3, d1)
    centre = jnp.where(positive, q2, q3)
    sa, sb, sc = e2 - e1, e3 - e2, e4 - e3
    eps = 4.0 * WENO_EPS
    k = 13.0 / 3.0
    x0 = 3.0 * e2 - e1
    x1 = e2 + e3
    x2 = 3.0 * e3 - e4
    y0 = (k * sa) * sa + (x0 * x0 + eps)
    y1 = (k * sb) * sb + (x1 * x1 + eps)
    y2 = (k * sc) * sc + (x2 * x2 + eps)
    m0, m1, m2 = y1 * y2, y0 * y2, y0 * y1
    w0 = m0 * m0
    w1 = 6.0 * (m1 * m1)
    w2 = 3.0 * (m2 * m2)
    bottom = w0 + w1 + w2
    first = w0 * (sb - sa)
    top = first + first + w2 * (sc - sb)
    return speed * centre + weight * ((x1 + e3) - top / bottom)


def kernel(n_gx, n_gy, depth, fields, coriolis, east, north, out,
           A, acc, dm, dp, dux, dvx, EA, SX, RX, YH, DR, DP, T0, T1, R1, R2,
           in_sem, y_send, y_recv, x_send, x_recv, d_send, d_recv, t_send, t_recv, s_send, s_recv):
    gx = lax.axis_index("gx")
    gy = lax.axis_index("gy")
    tiles = depth // ROWS
    diag = [(1, 1), (1, -1), (-1, 1), (-1, -1)]

    def exists(dx, dy):
        cond = None
        for pos, d, n in ((gx, dx, n_gx), (gy, dy, n_gy)):
            if d == 0:
                continue
            c = (pos + d < n) if d > 0 else (pos + d >= 0)
            cond = c if cond is None else jnp.logical_and(cond, c)
        return cond

    def target(dx, dy):
        return {"gx": gx + dx, "gy": gy + dy}

    loads = []
    for q in (3, 0, 1, 2, 4):
        c = pltpu.make_async_copy(fields.at[q], A.at[q], in_sem.at[q])
        c.start()
        loads.append(c)

    barrier = pltpu.get_barrier_semaphore()
    for k in range(1, n_gx):
        pl.semaphore_signal(barrier, inc=1, device_id={"gx": lax.rem(gx + k, n_gx)}, device_id_type=MESH)
    for k in range(1, n_gy):
        pl.semaphore_signal(barrier, inc=1, device_id={"gy": lax.rem(gy + k, n_gy)}, device_id_type=MESH)
    expected = jnp.int32(n_gx - 1 + n_gy - 1)
    for d in diag:
        cond = exists(*d)

        @pl.when(cond)
        def _():
            pl.semaphore_signal(barrier, inc=1, device_id=target(*d), device_id_type=MESH)

        expected = expected + cond.astype(jnp.int32)

    lane = lax.broadcasted_iota(jnp.int32, (ROWS, LANES), 1)
    sub = lax.broadcasted_iota(jnp.int32, (ROWS, LANES), 0)

    def tile(ref, q, z):
        return ref[q, z]

    def strided(ref, q, zt, y):
        return ref[q, pl.ds(zt * ROWS, ROWS), y]

    for c in loads:
        c.wait()

    packed_sum = jnp.zeros((ROWS, LANES), jnp.float32)
    for zt in range(tiles):
        total = A[3, zt * ROWS:(zt + 1) * ROWS, 0]
        for y in range(1, ROWS):
            total = total + A[3, zt * ROWS:(zt + 1) * ROWS, y]
        packed_sum = jnp.where(lane == zt, jnp.sum(total, axis=1, keepdims=True), packed_sum)
    T0[...] = packed_sum

    group = lane // 4
    spot = lane % 4
    for q in range(5):
        def pack(z, carry):
            left, right = carry
            t = tile(A, q, z)
            here = jnp.logical_and(group == z, spot < 3)
            left = jnp.where(here, pltpu.roll(t, 4 * z, 1), left)
            right = jnp.where(here, pltpu.roll(t, lax.rem(4 * z + 3, LANES), 1), right)
            return left, right
        zero = jnp.zeros((ROWS, LANES), jnp.float32)
        left, right = lax.fori_loop(0, depth, pack, (zero, zero), unroll=8)
        SX[0, q] = left
        SX[1, q] = right

    pl.semaphore_wait(barrier, expected)

    moves = []

    def message(dx, dy, src, dst, ssem, rsem):
        c = pltpu.make_async_remote_copy(src_ref=src, dst_ref=dst, send_sem=ssem, recv_sem=rsem,
                                         device_id=target(dx, dy), device_id_type=MESH)
        send_if, recv_if = exists(dx, dy), exists(-dx, -dy)

        @pl.when(send_if)
        def _():
            c.start()

        moves.append((send_if, c))

        def arrive():
            @pl.when(recv_if)
            def _():
                c.wait_recv()

            @pl.when(jnp.logical_not(recv_if))
            def _():
                dst[...] = jnp.zeros(dst.shape, jnp.float32)

        return arrive

    y_arrive, x_arrive, d_arrive = [], [], []
    for side, dx in ((0, 1), (1, -1)):
        for j in range(3):
            row = ROWS - 3 + j if dx == 1 else j
            near = j == 2 if dx == 1 else j == 0
            count = 5 if near else 4
            y_arrive.append(message(dx, 0, fields.at[pl.ds(0, count), :, row], YH.at[side, j, pl.ds(0, count)],
                                    y_send.at[side, j], y_recv.at[side, j]))
    for side, dy in ((0, 1), (1, -1)):
        x_arrive.append(message(0, dy, SX.at[1 - side], RX.at[side], x_send.at[side], x_recv.at[side]))
    for i, (dx, dy) in enumerate(diag):
        a, b = (0 if dx == 1 else 1), (0 if dy == 1 else 1)
        row = ROWS - 1 if dx == 1 else 0
        d_arrive.append(message(dx, dy, fields.at[pl.ds(0, 2), :, row], DR.at[a, b], d_send.at[0, i], d_recv.at[0, i]))
        d_arrive.append(message(dx, dy, SX.at[1 - b, pl.ds(0, 2)], DP.at[a, b], d_send.at[1, i], d_recv.at[1, i]))
    stage1 = []
    for k in range(1, n_gx):
        c = pltpu.make_async_remote_copy(src_ref=T0, dst_ref=R1.at[k - 1], send_sem=t_send.at[k - 1],
                                         recv_sem=t_recv.at[k - 1],
                                         device_id={"gx": lax.rem(gx + k, n_gx)}, device_id_type=MESH)
        c.start()
        stage1.append(c)

    turning = jnp.zeros((ROWS, LANES), jnp.float32)
    for y in range(ROWS):
        turning = jnp.where(sub == y, coriolis[y], turning)
    turning = SECTION_DT * turning
    east_dt = HALF_DT * east[...]
    north_dt = HALF_DT * north[...]

    def vertical(z, lower):
        at = [jnp.clip(z + o, 0, depth - 1) for o in (-2, -1, 0, 1, 2, 3)]
        speed = HALF_DT * (tile(A, 2, z) + tile(A, 2, at[3]))
        speed = speed * (z < depth - 1).astype(jnp.float32)
        positive = speed > 0.0
        weight = jnp.abs(speed) * (1.0 / 6.0)
        pz = tile(A, 4, at[3]) - tile(A, 4, at[1])
        factor = 1.0 - (z.astype(jnp.float32) + 0.5) / depth
        u, v = tile(A, 0, z), tile(A, 1, z)
        scaled = pz * factor
        force = (scaled * east_dt + turning * v, scaled * north_dt - turning * u, -HALF_DT * pz, None)
        uppers = []
        for q in range(4):
            cells = [tile(A, q, a) for a in at]
            upper = weno_flux(cells, positive, speed, weight)
            value = cells[2] - (upper - lower[q])
            if force[q] is not None:
                value = value + force[q]
            acc[q, z] = value
            uppers.append(upper)
        return tuple(uppers)

    zero = jnp.zeros((ROWS, LANES), jnp.float32)
    lax.fori_loop(0, depth, vertical, (zero,) * 4)

    for c in stage1:
        c.wait_recv()
    summed = T0[...]
    for k in range(n_gx - 1):
        summed = summed + R1[k]
    T1[...] = summed
    stage2 = []
    for k in range(1, n_gy):
        c = pltpu.make_async_remote_copy(src_ref=T1, dst_ref=R2.at[k - 1], send_sem=s_send.at[k - 1],
                                         recv_sem=s_recv.at[k - 1],
                                         device_id={"gy": lax.rem(gy + k, n_gy)}, device_id_type=MESH)
        c.start()
        stage2.append(c)

    for arrive in x_arrive:
        arrive()

    def shift(x, j, axis=1):
        n = x.shape[axis]
        return pltpu.roll(x, (-j) % n, axis)

    extra = []
    u_last = shift(SX[1, 0], 2)
    speed_e = HALF_DT * (u_last + RX[1, 0])
    positive_e = speed_e > 0.0
    weight_e = jnp.abs(speed_e) * (1.0 / 6.0)
    for q in range(4):
        own, far = SX[1, q], RX[1, q]
        cells = [own, shift(own, 1), shift(own, 2), far, shift(far, 1), shift(far, 2)]
        extra.append(weno_flux(cells, positive_e, speed_e, weight_e))

    def horizontal(z, carry):
        to_low = lax.rem(2 * LANES - 4 * z - 3, LANES)
        to_high = lax.rem(LANES - 4 * z, LANES)

        def moved(q, t, low, high):
            rl = pltpu.roll(RX[0, q], to_low, 1)
            rr = pltpu.roll(RX[1, q], to_high, 1)
            down = [pltpu.roll(jnp.where(lane >= LANES - j, rl, t), j, 1) for j in range(low, 0, -1)]
            up = [pltpu.roll(jnp.where(lane < j, rr, t), LANES - j, 1) for j in range(1, high + 1)]
            return down + [t] + up

        speed = positive = weight = None
        for q in range(4):
            cells = moved(q, tile(A, q, z), 3, 2)
            if q == 0:
                speed = HALF_DT * (cells[2] + cells[3])
                positive = speed > 0.0
                weight = jnp.abs(speed) * (1.0 / 6.0)
                dux[z] = cells[4] - cells[2]
            if q == 1:
                dvx[z] = cells[4] - cells[2]
            flux = weno_flux(cells, positive, speed, weight)
            past = jnp.where(lane == 0, pltpu.roll(extra[q], to_high, 1), flux)
            change = pltpu.roll(past, LANES - 1, 1) - flux
            if q == 0:
                pcells = moved(4, tile(A, 4, z), 1, 1)
                change = change + HALF_DT * (pcells[2] - pcells[0])
            acc[q, z] = acc[q, z] - change
            dm[q, z] = cells[3] - cells[2]
            dp[q, z] = cells[4] - cells[3]
        return carry

    lax.fori_loop(0, depth, horizontal, 0)

    for arrive in y_arrive + d_arrive:
        arrive()
    for c in stage2:
        c.wait_recv()
    mean = T1[...]
    for k in range(n_gy - 1):
        mean = mean + R2[k]
    mean = mean * (1.0 / (ROWS * LANES * n_gx * n_gy))

    scale = HALF_DT * SMAG_COEF

    def mixing_coefficient(ux, vy, uy, vx):
        cross = uy + vx
        return scale * jnp.sqrt(0.5 * (ux * ux + vy * vy) + (0.25 * (cross * cross) + BACKGROUND))

    def along_y(zt, carry):
        levels = pl.ds(pl.multiple_of(zt * ROWS, ROWS), ROWS)

        def row(q, y):
            if y < 0:
                return YH[0, y + 3, q, levels]
            if y >= ROWS:
                return YH[1, y - ROWS, q, levels]
            return A[q, levels, y]

        us = {y: row(0, y) for y in range(-2, ROWS + 2)}
        vs = {y: row(1, y) for y in range(-2, ROWS + 2)}
        eddy = []
        for y in range(-1, ROWS + 1):
            if 0 <= y < ROWS:
                ux, vx = dux[levels, y], dvx[levels, y]
            else:
                a = 0 if y < 0 else 1
                both = []
                for q, base in ((0, us[y]), (1, vs[y])):
                    right = pltpu.roll(jnp.where(lane == 0, DR[a, 1, q, levels], base), LANES - 1, 1)
                    left = pltpu.roll(jnp.where(lane == LANES - 1, DR[a, 0, q, levels], base), 1, 1)
                    both.append(right - left)
                ux, vx = both
            e = mixing_coefficient(ux, vs[y + 1] - vs[y - 1], us[y + 1] - us[y - 1], vx)
            eddy.append(e)
            if 0 <= y < ROWS:
                EA[levels, y] = e
        speeds, signs, weights, spread = [], [], [], []
        for f in range(ROWS + 1):
            s = HALF_DT * (vs[f - 1] + vs[f])
            speeds.append(s)
            signs.append(s > 0.0)
            weights.append(jnp.abs(s) * (1.0 / 6.0))
            spread.append(eddy[f] + eddy[f + 1])
        level_mean = jnp.sum(jnp.where(lane == zt, mean, 0.0), axis=1, keepdims=True)
        for q in range(4):
            cells = [row(q, y) for y in range(-3, ROWS + 3)]
            lower = None
            for f in range(ROWS + 1):
                six = cells[f:f + 6]
                flux = weno_flux(six, signs[f], speeds[f], weights[f]) - spread[f] * (six[3] - six[2])
                if f:
                    y = f - 1
                    value = acc[q, levels, y] - (flux - lower)
                    if q == 1:
                        value = value - HALF_DT * (row(4, y + 1) - row(4, y - 1))
                    if q == 2:
                        value = value + (SECTION_DT * BUOYANCY) * (row(3, y) - level_mean)
                    acc[q, levels, y] = value
                lower = flux
        return carry

    lax.fori_loop(0, tiles, along_y, 0)

    def outside(side):
        parts = []
        for q in range(2):
            far, own = RX[side, q], SX[side, q]
            if side == 0:
                plus, base, minus = own, shift(far, 2), shift(far, 1)
                above, below = shift(DP[1, 0, q], 2), shift(DP[0, 0, q], 2)
            else:
                plus, base, minus = shift(far, 1), far, shift(own, 2)
                above, below = DP[1, 1, q], DP[0, 1, q]
            nxt = pltpu.roll(jnp.where(sub == 0, above, base), ROWS - 1, 0)
            prv = pltpu.roll(jnp.where(sub == ROWS - 1, below, base), 1, 0)
            parts.append((plus - minus, nxt - prv))
        (ux, uy), (vx, vy) = parts
        return mixing_coefficient(ux, vy, uy, vx)

    e_low, e_high = outside(0), outside(1)

    def final(z, carry):
        e = EA[z]
        low = pltpu.roll(e_low, lax.rem(2 * LANES - 4 * z - 1, LANES), 1)
        high = pltpu.roll(e_high, lax.rem(LANES - 4 * z, LANES), 1)
        before = e + pltpu.roll(jnp.where(lane == LANES - 1, low, e), 1, 1)
        after = e + pltpu.roll(jnp.where(lane == 0, high, e), LANES - 1, 1)
        for q in range(4):
            out[q, z] = acc[q, z] + (after * dp[q, z] - before * dm[q, z])
        return carry

    lax.fori_loop(0, depth, final, 0, unroll=4)

    for cond, c in moves:
        @pl.when(cond)
        def _():
            c.wait_send()
    for c in stage1 + stage2:
        c.wait_send()


def body(n_gx, n_gy, fields, coriolis, slope_east, slope_north):
    depth = fields.shape[1]
    f32 = jnp.float32
    block = (depth, ROWS, LANES)
    dma = pltpu.SemaphoreType.DMA
    vmem = pl.BlockSpec(memory_space=pltpu.VMEM)
    return pl.pallas_call(
        functools.partial(kernel, n_gx, n_gy, depth),
        out_shape=jax.ShapeDtypeStruct((4,) + block, f32),
        in_specs=[pl.BlockSpec(memory_space=pl.ANY), pl.BlockSpec(memory_space=pltpu.SMEM), vmem, vmem],
        out_specs=vmem,
        scratch_shapes=[
            pltpu.VMEM((5,) + block, f32),
            pltpu.VMEM((4,) + block, f32),
            pltpu.VMEM((4,) + block, f32),
            pltpu.VMEM((4,) + block, f32),
            pltpu.VMEM(block, f32),
            pltpu.VMEM(block, f32),
            pltpu.VMEM(block, f32),
            pltpu.VMEM((2, 5, ROWS, LANES), f32),
            pltpu.VMEM((2, 5, ROWS, LANES), f32),
            pltpu.VMEM((2, 3, 5, depth, LANES), f32),
            pltpu.VMEM((2, 2, 2, depth, LANES), f32),
            pltpu.VMEM((2, 2, 2, ROWS, LANES), f32),
            pltpu.VMEM((ROWS, LANES), f32),
            pltpu.VMEM((ROWS, LANES), f32),
            pltpu.VMEM((n_gx - 1, ROWS, LANES), f32),
            pltpu.VMEM((n_gy - 1, ROWS, LANES), f32),
            dma((5,)),
            dma((2, 3)), dma((2, 3)),
            dma((2,)), dma((2,)),
            dma((2, 4)), dma((2, 4)),
            dma((n_gx - 1,)), dma((n_gx - 1,)),
            dma((n_gy - 1,)), dma((n_gy - 1,)),
        ],
        compiler_params=pltpu.CompilerParams(collective_id=0, has_side_effects=True),
        name="section",
    )(fields, coriolis, slope_east, slope_north)


def solution(mesh):
    return jax.shard_map(
        functools.partial(body, mesh.shape["gx"], mesh.shape["gy"]),
        mesh=mesh,
        in_specs=(P(None, None, "gx", "gy"), P("gx"), P("gx", "gy"), P("gx", "gy")),
        out_specs=P(None, None, "gx", "gy"),
        check_vma=False,
    )
```

time: 87.4 us -> 34.4 us (0.39)
  the two profiles are of different devices: /device:TPU:1 before, /device:TPU:0 now
where the time goes in v1:
time: 34.4 us; the launch traced here: 34.2 us
  Pallas kernels  32.3 us (94%)
  local copies, waits for them, and re-layouts  1.87 us (5%)
    pallas_call x1, Pallas kernels, body(): pl.pallas_call(functools.partial(kernel, n_gx, n_gy, depth), out_shape=ja...  32.3 us
    unnamed x1, local copies, waits for them, and re-layouts  1.87 us

profile of v1, /device:TPU:0, one launch (start us, length us, event | category | flops | bytes accessed | tf_op | source)
XLA Modules:
  0.0 34.2 jit_solution(4211150792584708028)
XLA Ops:
  0.0 32.3 %section.1 = f32[4,32,8,128]{3,2,1,0:T(8,128)} custom-call(f32[5,32,8,128]{3,2,1,0:T(8,128)} %fields.1, f32[8]{0:T(128)} %coriolis.1, f32[8,128]{1,0:T(8,128)} %east.1, f32[8,128]{1,0:T(8,128)} %north.1), custom_call_target="tpu_custom_call" | custom-call | tf_op jit(solution)/shard_map/section/pallas_call | solution.py:384
  32.4 1.9 %copy.6 = f32[4,32,8,128]{3,2,1,0:T(8,128)} copy(f32[4,32,8,128]{3,2,1,0:T(8,128)} %section.1) | data formatting | bytes 1048576

commit v2 on v1

--- a/solution.py
+++ b/solution.py
@@ -46,7 +46,7 @@
 
 
 def kernel(n_gx, n_gy, depth, fields, coriolis, east, north, out,
-           A, acc, dm, dp, dux, dvx, EA, SX, RX, YH, DR, DP, T0, T1, R1, R2,
+           A, acc, dm, dp, dux, dvx, EA, SX, RX, YS, YH, DS, DR, MB, T0, T1, R1, R2,
            in_sem, y_send, y_recv, x_send, x_recv, d_send, d_recv, t_send, t_recv, s_send, s_recv):
     gx = lax.axis_index("gx")
     gy = lax.axis_index("gy")
@@ -92,17 +92,21 @@
     def tile(ref, q, z):
         return ref[q, z]
 
-    def strided(ref, q, zt, y):
-        return ref[q, pl.ds(zt * ROWS, ROWS), y]
+    flat4 = lambda ref: ref.reshape(ref.shape[0], depth * ROWS, LANES)
+    flat3 = lambda ref: ref.reshape(depth * ROWS, LANES)
+    Af, accf, duxf, dvxf, EAf = flat4(A), flat4(acc), flat3(dux), flat3(dvx), flat3(EA)
+
+    def every(zt, y):
+        return pl.ds(zt * ROWS * ROWS + y, ROWS, stride=ROWS)
 
     for c in loads:
         c.wait()
 
     packed_sum = jnp.zeros((ROWS, LANES), jnp.float32)
     for zt in range(tiles):
-        total = A[3, zt * ROWS:(zt + 1) * ROWS, 0]
+        total = Af[3, every(zt, 0)]
         for y in range(1, ROWS):
-            total = total + A[3, zt * ROWS:(zt + 1) * ROWS, y]
+            total = total + Af[3, every(zt, y)]
         packed_sum = jnp.where(lane == zt, jnp.sum(total, axis=1, keepdims=True), packed_sum)
     T0[...] = packed_sum
 
@@ -121,6 +125,31 @@
         SX[0, q] = left
         SX[1, q] = right
 
+    def slot(j, q):
+        return 4 * j + q if q < 4 else 12
+
+    for side in range(2):
+        near = 0 if side == 0 else ROWS - 1
+        for q in range(5):
+            for j in (range(3) if q < 4 else (0,)):
+                row = near + j if side == 0 else near - j
+                for zt in range(tiles):
+                    YS[side, slot(j, q), zt * ROWS:(zt + 1) * ROWS] = Af[q, every(zt, row)]
+
+    for a in range(2):
+        row = ROWS - 1 if a == 0 else 0
+        for b in range(2):
+            column = LANES - 1 if b == 0 else 0
+            packed = jnp.zeros((ROWS, LANES), jnp.float32)
+            for zt in range(tiles):
+                for q in range(2):
+                    t = Af[q, every(zt, row)]
+                    goal = 2 * zt + q
+                    packed = jnp.where(lane == goal, pltpu.roll(t, (goal - column) % LANES, 1), packed)
+            DS[a, b, 0] = packed
+            DS[a, b, 1] = SX[1 - b, 0]
+            DS[a, b, 2] = SX[1 - b, 1]
+
     pl.semaphore_wait(barrier, expected)
 
     moves = []
@@ -149,19 +178,12 @@
 
     y_arrive, x_arrive, d_arrive = [], [], []
     for side, dx in ((0, 1), (1, -1)):
-        for j in range(3):
-            row = ROWS - 3 + j if dx == 1 else j
-            near = j == 2 if dx == 1 else j == 0
-            count = 5 if near else 4
-            y_arrive.append(message(dx, 0, fields.at[pl.ds(0, count), :, row], YH.at[side, j, pl.ds(0, count)],
-                                    y_send.at[side, j], y_recv.at[side, j]))
+        y_arrive.append(message(dx, 0, YS.at[1 - side], YH.at[side], y_send.at[side], y_recv.at[side]))
     for side, dy in ((0, 1), (1, -1)):
         x_arrive.append(message(0, dy, SX.at[1 - side], RX.at[side], x_send.at[side], x_recv.at[side]))
     for i, (dx, dy) in enumerate(diag):
         a, b = (0 if dx == 1 else 1), (0 if dy == 1 else 1)
-        row = ROWS - 1 if dx == 1 else 0
-        d_arrive.append(message(dx, dy, fields.at[pl.ds(0, 2), :, row], DR.at[a, b], d_send.at[0, i], d_recv.at[0, i]))
-        d_arrive.append(message(dx, dy, SX.at[1 - b, pl.ds(0, 2)], DP.at[a, b], d_send.at[1, i], d_recv.at[1, i]))
+        d_arrive.append(message(dx, dy, DS.at[a, b], DR.at[a, b], d_send.at[i], d_recv.at[i]))
     stage1 = []
     for k in range(1, n_gx):
         c = pltpu.make_async_remote_copy(src_ref=T0, dst_ref=R1.at[k - 1], send_sem=t_send.at[k - 1],
@@ -269,13 +291,6 @@
 
     for arrive in y_arrive + d_arrive:
         arrive()
-    for c in stage2:
-        c.wait_recv()
-    mean = T1[...]
-    for k in range(n_gy - 1):
-        mean = mean + R2[k]
-    mean = mean * (1.0 / (ROWS * LANES * n_gx * n_gy))
-
     scale = HALF_DT * SMAG_COEF
 
     def mixing_coefficient(ux, vy, uy, vx):
@@ -287,29 +302,29 @@
 
         def row(q, y):
             if y < 0:
-                return YH[0, y + 3, q, levels]
+                return YH[0, slot(-1 - y, q), levels]
             if y >= ROWS:
-                return YH[1, y - ROWS, q, levels]
-            return A[q, levels, y]
+                return YH[1, slot(y - ROWS, q), levels]
+            return Af[q, every(zt, y)]
 
         us = {y: row(0, y) for y in range(-2, ROWS + 2)}
         vs = {y: row(1, y) for y in range(-2, ROWS + 2)}
         eddy = []
         for y in range(-1, ROWS + 1):
             if 0 <= y < ROWS:
-                ux, vx = dux[levels, y], dvx[levels, y]
+                ux, vx = duxf[every(zt, y)], dvxf[every(zt, y)]
             else:
                 a = 0 if y < 0 else 1
                 both = []
                 for q, base in ((0, us[y]), (1, vs[y])):
-                    right = pltpu.roll(jnp.where(lane == 0, DR[a, 1, q, levels], base), LANES - 1, 1)
-                    left = pltpu.roll(jnp.where(lane == LANES - 1, DR[a, 0, q, levels], base), 1, 1)
+                    right = pltpu.roll(jnp.where(lane == 0, pltpu.roll(DR[a, 1, 0], lax.rem(LANES - 2 * zt - q, LANES), 1), base), LANES - 1, 1)
+                    left = pltpu.roll(jnp.where(lane == LANES - 1, pltpu.roll(DR[a, 0, 0], LANES - 1 - 2 * zt - q, 1), base), 1, 1)
                     both.append(right - left)
                 ux, vx = both
             e = mixing_coefficient(ux, vs[y + 1] - vs[y - 1], us[y + 1] - us[y - 1], vx)
             eddy.append(e)
             if 0 <= y < ROWS:
-                EA[levels, y] = e
+                EAf[every(zt, y)] = e
         speeds, signs, weights, spread = [], [], [], []
         for f in range(ROWS + 1):
             s = HALF_DT * (vs[f - 1] + vs[f])
@@ -317,7 +332,6 @@
             signs.append(s > 0.0)
             weights.append(jnp.abs(s) * (1.0 / 6.0))
             spread.append(eddy[f] + eddy[f + 1])
-        level_mean = jnp.sum(jnp.where(lane == zt, mean, 0.0), axis=1, keepdims=True)
         for q in range(4):
             cells = [row(q, y) for y in range(-3, ROWS + 3)]
             lower = None
@@ -326,12 +340,12 @@
                 flux = weno_flux(six, signs[f], speeds[f], weights[f]) - spread[f] * (six[3] - six[2])
                 if f:
                     y = f - 1
-                    value = acc[q, levels, y] - (flux - lower)
+                    value = accf[q, every(zt, y)] - (flux - lower)
                     if q == 1:
                         value = value - HALF_DT * (row(4, y + 1) - row(4, y - 1))
                     if q == 2:
-                        value = value + (SECTION_DT * BUOYANCY) * (row(3, y) - level_mean)
-                    acc[q, levels, y] = value
+                        value = value + (SECTION_DT * BUOYANCY) * row(3, y)
+                    accf[q, every(zt, y)] = value
                 lower = flux
         return carry
 
@@ -343,10 +357,10 @@
             far, own = RX[side, q], SX[side, q]
             if side == 0:
                 plus, base, minus = own, shift(far, 2), shift(far, 1)
-                above, below = shift(DP[1, 0, q], 2), shift(DP[0, 0, q], 2)
+                above, below = shift(DR[1, 0, q + 1], 2), shift(DR[0, 0, q + 1], 2)
             else:
                 plus, base, minus = shift(far, 1), far, shift(own, 2)
-                above, below = DP[1, 1, q], DP[0, 1, q]
+                above, below = DR[1, 1, q + 1], DR[0, 1, q + 1]
             nxt = pltpu.roll(jnp.where(sub == 0, above, base), ROWS - 1, 0)
             prv = pltpu.roll(jnp.where(sub == ROWS - 1, below, base), 1, 0)
             parts.append((plus - minus, nxt - prv))
@@ -354,6 +368,17 @@
         return mixing_coefficient(ux, vy, uy, vx)
 
     e_low, e_high = outside(0), outside(1)
+
+    for c in stage2:
+        c.wait_recv()
+    mean = T1[...]
+    for k in range(n_gy - 1):
+        mean = mean + R2[k]
+    mean = mean * (1.0 / (ROWS * LANES * n_gx * n_gy))
+    mean = (SECTION_DT * BUOYANCY) * mean
+    for zt in range(tiles):
+        level = jnp.sum(jnp.where(lane == zt, mean, 0.0), axis=1, keepdims=True)
+        MB[zt * ROWS:(zt + 1) * ROWS] = jnp.broadcast_to(level, (ROWS, LANES))
 
     def final(z, carry):
         e = EA[z]
@@ -362,7 +387,10 @@
         before = e + pltpu.roll(jnp.where(lane == LANES - 1, low, e), 1, 1)
         after = e + pltpu.roll(jnp.where(lane == 0, high, e), LANES - 1, 1)
         for q in range(4):
-            out[q, z] = acc[q, z] + (after * dp[q, z] - before * dm[q, z])
+            value = acc[q, z] + (after * dp[q, z] - before * dm[q, z])
+            if q == 2:
+                value = value - MB[pl.ds(z, 1)]
+            out[q, z] = value
         return carry
 
     lax.fori_loop(0, depth, final, 0, unroll=4)
@@ -396,17 +424,19 @@
             pltpu.VMEM(block, f32),
             pltpu.VMEM((2, 5, ROWS, LANES), f32),
             pltpu.VMEM((2, 5, ROWS, LANES), f32),
-            pltpu.VMEM((2, 3, 5, depth, LANES), f32),
-            pltpu.VMEM((2, 2, 2, depth, LANES), f32),
-            pltpu.VMEM((2, 2, 2, ROWS, LANES), f32),
+            pltpu.VMEM((2, 13, depth, LANES), f32),
+            pltpu.VMEM((2, 13, depth, LANES), f32),
+            pltpu.VMEM((2, 2, 3, ROWS, LANES), f32),
+            pltpu.VMEM((2, 2, 3, ROWS, LANES), f32),
+            pltpu.VMEM((depth, LANES), f32),
             pltpu.VMEM((ROWS, LANES), f32),
             pltpu.VMEM((ROWS, LANES), f32),
             pltpu.VMEM((n_gx - 1, ROWS, LANES), f32),
             pltpu.VMEM((n_gy - 1, ROWS, LANES), f32),
             dma((5,)),
-            dma((2, 3)), dma((2, 3)),
             dma((2,)), dma((2,)),
-            dma((2, 4)), dma((2, 4)),
+            dma((2,)), dma((2,)),
+            dma((4,)), dma((4,)),
             dma((n_gx - 1,)), dma((n_gx - 1,)),
             dma((n_gy - 1,)), dma((n_gy - 1,)),
         ],

time: 34.4 us -> 27 us (0.78)
  Pallas kernels: 32.3 us -> 24.9 us
    pallas_call x1, Pallas kernels: 32.3 us -> 24.9 us  [body(): pl.pallas_call(functools.partial(kernel, n_gx, n_gy, depth), out_shape=ja...]
where the time goes in v2:
time: 27 us; the launch traced here: 26.8 us
  Pallas kernels  24.9 us (92%)
  local copies, waits for them, and re-layouts  1.87 us (7%)
    pallas_call x1, Pallas kernels, body(): pl.pallas_call(functools.partial(kernel, n_gx, n_gy, depth), out_shape=ja...  24.9 us
    unnamed x1, local copies, waits for them, and re-layouts  1.87 us

profile of v2, /device:TPU:0, one launch (start us, length us, event | category | flops | bytes accessed | tf_op | source)
XLA Modules:
  0.0 26.8 jit_solution(6971443319121052128)
XLA Ops:
  0.0 24.9 %section.1 = f32[4,32,8,128]{3,2,1,0:T(8,128)} custom-call(f32[5,32,8,128]{3,2,1,0:T(8,128)} %fields.1, f32[8]{0:T(128)} %coriolis.1, f32[8,128]{1,0:T(8,128)} %east.1, f32[8,128]{1,0:T(8,128)} %north.1), custom_call_target="tpu_custom_call" | custom-call | tf_op jit(solution)/shard_map/section/pallas_call | solution.py:412
  24.9 1.9 %copy.6 = f32[4,32,8,128]{3,2,1,0:T(8,128)} copy(f32[4,32,8,128]{3,2,1,0:T(8,128)} %section.1) | data formatting | bytes 1048576

commit v3 on v2

--- a/solution.py
+++ b/solution.py
@@ -150,48 +150,6 @@
             DS[a, b, 1] = SX[1 - b, 0]
             DS[a, b, 2] = SX[1 - b, 1]
 
-    pl.semaphore_wait(barrier, expected)
-
-    moves = []
-
-    def message(dx, dy, src, dst, ssem, rsem):
-        c = pltpu.make_async_remote_copy(src_ref=src, dst_ref=dst, send_sem=ssem, recv_sem=rsem,
-                                         device_id=target(dx, dy), device_id_type=MESH)
-        send_if, recv_if = exists(dx, dy), exists(-dx, -dy)
-
-        @pl.when(send_if)
-        def _():
-            c.start()
-
-        moves.append((send_if, c))
-
-        def arrive():
-            @pl.when(recv_if)
-            def _():
-                c.wait_recv()
-
-            @pl.when(jnp.logical_not(recv_if))
-            def _():
-                dst[...] = jnp.zeros(dst.shape, jnp.float32)
-
-        return arrive
-
-    y_arrive, x_arrive, d_arrive = [], [], []
-    for side, dx in ((0, 1), (1, -1)):
-        y_arrive.append(message(dx, 0, YS.at[1 - side], YH.at[side], y_send.at[side], y_recv.at[side]))
-    for side, dy in ((0, 1), (1, -1)):
-        x_arrive.append(message(0, dy, SX.at[1 - side], RX.at[side], x_send.at[side], x_recv.at[side]))
-    for i, (dx, dy) in enumerate(diag):
-        a, b = (0 if dx == 1 else 1), (0 if dy == 1 else 1)
-        d_arrive.append(message(dx, dy, DS.at[a, b], DR.at[a, b], d_send.at[i], d_recv.at[i]))
-    stage1 = []
-    for k in range(1, n_gx):
-        c = pltpu.make_async_remote_copy(src_ref=T0, dst_ref=R1.at[k - 1], send_sem=t_send.at[k - 1],
-                                         recv_sem=t_recv.at[k - 1],
-                                         device_id={"gx": lax.rem(gx + k, n_gx)}, device_id_type=MESH)
-        c.start()
-        stage1.append(c)
-
     turning = jnp.zeros((ROWS, LANES), jnp.float32)
     for y in range(ROWS):
         turning = jnp.where(sub == y, coriolis[y], turning)
@@ -224,6 +182,48 @@
     zero = jnp.zeros((ROWS, LANES), jnp.float32)
     lax.fori_loop(0, depth, vertical, (zero,) * 4)
 
+    pl.semaphore_wait(barrier, expected)
+
+    moves = []
+
+    def message(dx, dy, src, dst, ssem, rsem):
+        c = pltpu.make_async_remote_copy(src_ref=src, dst_ref=dst, send_sem=ssem, recv_sem=rsem,
+                                         device_id=target(dx, dy), device_id_type=MESH)
+        send_if, recv_if = exists(dx, dy), exists(-dx, -dy)
+
+        @pl.when(send_if)
+        def _():
+            c.start()
+
+        moves.append((send_if, c))
+
+        def arrive():
+            @pl.when(recv_if)
+            def _():
+                c.wait_recv()
+
+            @pl.when(jnp.logical_not(recv_if))
+            def _():
+                dst[...] = jnp.zeros(dst.shape, jnp.float32)
+
+        return arrive
+
+    stage1 = []
+    for k in range(1, n_gx):
+        c = pltpu.make_async_remote_copy(src_ref=T0, dst_ref=R1.at[k - 1], send_sem=t_send.at[k - 1],
+                                         recv_sem=t_recv.at[k - 1],
+                                         device_id={"gx": lax.rem(gx + k, n_gx)}, device_id_type=MESH)
+        c.start()
+        stage1.append(c)
+
+    y_arrive, x_arrive, d_arrive = [], [], []
+    for side, dx in ((0, 1), (1, -1)):
+        y_arrive.append(message(dx, 0, YS.at[1 - side], YH.at[side], y_send.at[side], y_recv.at[side]))
+    for side, dy in ((0, 1), (1, -1)):
+        x_arrive.append(message(0, dy, SX.at[1 - side], RX.at[side], x_send.at[side], x_recv.at[side]))
+    for i, (dx, dy) in enumerate(diag):
+        a, b = (0 if dx == 1 else 1), (0 if dy == 1 else 1)
+        d_arrive.append(message(dx, dy, DS.at[a, b], DR.at[a, b], d_send.at[i], d_recv.at[i]))
     for c in stage1:
         c.wait_recv()
     summed = T0[...]

time: 27 us -> 24.9 us (0.922)
  Pallas kernels: 24.9 us -> 22.9 us
    pallas_call x1, Pallas kernels: 24.9 us -> 22.9 us  [body(): pl.pallas_call(functools.partial(kernel, n_gx, n_gy, depth), out_shape=ja...]
where the time goes in v3:
time: 24.9 us; the launch traced here: 24.7 us
  Pallas kernels  22.9 us (92%)
  local copies, waits for them, and re-layouts  1.87 us (8%)
    pallas_call x1, Pallas kernels, body(): pl.pallas_call(functools.partial(kernel, n_gx, n_gy, depth), out_shape=ja...  22.9 us
    unnamed x1, local copies, waits for them, and re-layouts  1.87 us

profile of v3, /device:TPU:0, one launch (start us, length us, event | category | flops | bytes accessed | tf_op | source)
XLA Modules:
  0.0 24.7 jit_solution(14963401801443590175)
XLA Ops:
  0.0 22.9 %section.1 = f32[4,32,8,128]{3,2,1,0:T(8,128)} custom-call(f32[5,32,8,128]{3,2,1,0:T(8,128)} %fields.1, f32[8]{0:T(128)} %coriolis.1, f32[8,128]{1,0:T(8,128)} %east.1, f32[8,128]{1,0:T(8,128)} %north.1), custom_call_target="tpu_custom_call" | custom-call | tf_op jit(solution)/shard_map/section/pallas_call | solution.py:412
  22.9 1.9 %copy.6 = f32[4,32,8,128]{3,2,1,0:T(8,128)} copy(f32[4,32,8,128]{3,2,1,0:T(8,128)} %section.1) | data formatting | bytes 1048576
